TPU v7x, 32 devices: a whole 2x2x4 slice. The times are simulated.
32 devices in a mesh: dp: 4 (over x, core), tensor: 8 (over z, y).
Axes of the slice: x: 2, y: 2, z: 4, core: 2. Of those that a mesh axis runs over, the one named last changes fastest.
Arguments:
- activations: bfloat16 [1024, 5120], P('dp'), may hold values from -6 to 6
- grad_out: bfloat16 [1024, 5120], P('dp'), may hold values from -6 to 6
- gate_pre: bfloat16 [1024, 7168], P('dp', 'tensor'), may hold values from -8 to 8
- up_pre: bfloat16 [1024, 7168], P('dp', 'tensor'), may hold values from -6 to 6
- gate_up: bfloat16 [5120, 2, 7168], P('dp', None, 'tensor'), may hold values from -0.078125 to 0.078125
- down_weight: bfloat16 [5120, 7168], P('dp', 'tensor'), may hold values from -0.0625 to 0.0625
Outputs:
- grad_input: bfloat16 [1024, 5120], P('dp')
- grad_gate_up: float32 [5120, 2, 7168], P('dp', None, 'tensor')
- grad_down: float32 [5120, 7168], P('dp', 'tensor')
All inputs are finite; a program needn't handle non-finite values.
Results may differ from a plain program's by a relative error of at most 0.017.
Values may be sent and summed in bfloat16 or wider, within the bound.
A program may use at most 128 MiB of HBM per device.

v0:
```python
import jax
import jax.numpy as jnp
from jax import lax
from jax.sharding import PartitionSpec as P


def per_device(activations, grad_out, gate_pre, up_pre, gate_up, down_weight):
    tokens = activations.shape[0]
    hidden_width = down_weight.shape[1]
    dp_count = lax.axis_size("dp")
    slab_rows = down_weight.shape[0]
    gate_wide = gate_pre.astype(jnp.float32)
    up_wide = up_pre.astype(jnp.float32)
    gate_sigmoid = jax.nn.sigmoid(gate_wide)
    gate_silu = gate_wide * gate_sigmoid
    hidden = (gate_silu * up_wide).astype(jnp.bfloat16)
    grad_h = jnp.dot(
        grad_out,
        lax.all_gather(down_weight, "dp", axis=0, tiled=True),
        preferred_element_type=jnp.float32,
    )
    grad_gate = grad_h * up_wide * gate_sigmoid * (1.0 + gate_wide * (1.0 - gate_sigmoid))
    grad_up = grad_h * gate_silu
    grad_hidden = (
        jnp.stack([grad_gate, grad_up], axis=1)
        .astype(jnp.bfloat16)
        .reshape(tokens, 2 * hidden_width)
    )
    pieces = lax.all_gather(gate_up, "dp", axis=0, tiled=True)
    flattened = pieces.reshape(pieces.shape[0], 2 * hidden_width)
    partial_sum = lax.dot_general(
        grad_hidden, flattened, (((1,), (1,)), ((), ())), preferred_element_type=jnp.float32
    )
    share_block = lax.psum_scatter(
        partial_sum.astype(jnp.bfloat16), "tensor", scatter_dimension=0, tiled=True
    )
    grad_input = lax.all_gather(share_block, "tensor", axis=0, tiled=True)
    x_cols, dy_cols = (
        lax.all_to_all(activations, "dp", split_axis=1, concat_axis=0, tiled=True),
        lax.all_to_all(grad_out, "dp", split_axis=1, concat_axis=0, tiled=True),
    )
    stacked = jnp.concatenate([grad_hidden, hidden], axis=1)
    pieces = lax.all_gather(stacked, "dp", axis=0, tiled=True)
    groups = pieces.shape[0] // tokens
    left_cols = x_cols.reshape(groups, tokens, slab_rows)
    right_cols = dy_cols.reshape(groups, tokens, slab_rows)
    blocks = pieces.reshape(groups, tokens, 3 * hidden_width)
    gate_part = jnp.einsum(
        "gtn,gtk->gnk",
        left_cols,
        blocks[:, :, : 2 * hidden_width],
        preferred_element_type=jnp.float32,
    )
    down_part = jnp.einsum(
        "gtn,gtk->gnk",
        right_cols,
        blocks[:, :, 2 * hidden_width :],
        preferred_element_type=jnp.float32,
    )
    paired = jnp.concatenate([gate_part, down_part], axis=2)
    paired = lax.optimization_barrier(paired.astype(jnp.bfloat16))
    summed = jnp.sum(paired.astype(jnp.float32), axis=0)
    summed = summed / dp_count
    grad_gate_up = summed[:, : 2 * hidden_width].reshape(slab_rows, 2, hidden_width)
    grad_down = summed[:, 2 * hidden_width :]
    return (grad_input, grad_gate_up, grad_down)


def solution(mesh):
    in_specs = (
        P("dp", None),
        P("dp", None),
        P("dp", "tensor"),
        P("dp", "tensor"),
        P("dp", None, "tensor"),
        P("dp", "tensor"),
    )
    out_specs = (P("dp", None), P("dp", None, "tensor"), P("dp", "tensor"))
    return jax.shard_map(
        per_device, mesh=mesh, in_specs=in_specs, out_specs=out_specs, check_vma=False
    )
```

profile of v0, /device:TPU:0, one launch (start us, length us, event | category | flops | bytes accessed | tf_op | source)
XLA Modules:
  0.0 420.8 jit_solution(17504109902970205491)
XLA Ops:
  7.2 0.0 all-gather.5.cloned.1.call-start
  7.2 0.7 all-gather.5.cloned.1.call-update
  7.9 0.0 copy-start.3
  7.9 0.0 all-gather.7.cloned.1.call-start
  8.0 5.1 %copy.20 = bf16[1280,2,896]{2,0,1:T(8,128)(2,1)} copy(bf16[1280,2,896]{2,1,0:T(2,128)(2,1)} %param.10) | data formatting | bytes 9175040 | tf_op args[4]
  13.0 0.0 copy-start
  13.0 0.0 all-gather.7.cloned.1.call-update
  13.0 0.0 all-gather.11.cloned.1.call-start
  13.1 0.0 copy-done.3
  13.1 1.5 fusion.10
  14.6 0.2 copy.22
  14.8 60.2 %all-gather.5.cloned.1.call-done = bf16[5120,896]{1,0:T(8,128)(2,1)} async-done(((bf16[1280,896]{1,0:T(8,128)(2,1)}), bf16[5120,896]{1,0:T(8,128)(2,1)}) %all-gather.5.cloned.1.call-update) | async-done | bytes 9175056 | tf_op jit(solution)/shard_map/all_gather | solution.py:19
  75.0 0.0 copy-done
  75.0 6.9 %fusion.9 = (bf16[256,1,896]{2,0,1:T(8,128)(2,1)S(1)}, bf16[256,1,896]{2,0,1:T(8,128)(2,1)S(1)}) fusion(bf16[256,896]{1,0:T(8,128)(2,1)} %param.9, bf16[256,896]{1,0:T(8,128)(2,1)} %param.8, bf16[256,5120]{1,0:T(8,128)(2,1)S(1)} %copy-done, bf16[5120,896]{1,0:T(8,128)(2,1)} %all-gather.5.cloned.1.call-done), kind=kOutput, calls=%fused_computation.22 | convolution fusion | flops 2352250880 | bytes 13631488 | tf_op jit(solution)/shard_map/dot_general | solution.py:17
  82.0 0.0 copy-start.1
  82.0 0.8 copy-done.1
  82.7 0.1 maximum_convert_fusion
  82.8 0.0 copy-start.2
  82.8 0.5 copy.21
  83.4 1.2 pad_maximum_fusion.1
  84.6 0.0 all-gather.11.cloned.1.call-update
  84.6 0.0 reduce-scatter.2.cloned.1.call-start
  84.6 107.6 %all-gather.7.cloned.1.call-done = bf16[5120,2,896]{2,0,1:T(8,128)(2,1)} async-done(((bf16[1280,2,896]{2,0,1:T(8,128)(2,1)}), bf16[5120,2,896]{2,0,1:T(8,128)(2,1)}) %all-gather.7.cloned.1.call-update) | async-done | bytes 18350096 | tf_op jit(solution)/shard_map/all_gather | solution.py:29
  192.2 0.0 copy-done.2
  192.2 9.9 %fusion.2 = bf16[256,5120]{1,0:T(8,128)(2,1)} fusion(bf16[5120,2,896]{2,0,1:T(8,128)(2,1)} %all-gather.7.cloned.1.call-done, bf16[256,1,896]{2,0,1:T(8,128)(2,1)S(1)} %copy-done.2, bf16[256,1,896]{2,0,1:T(8,128)(2,1)S(1)} %get-tuple-element.6), kind=kOutput, calls=%fused_computation.8 | convolution fusion | flops 4699389952 | bytes 21889024 | tf_op jit(solution)/shard_map/dot_general | solution.py:31
  202.1 0.0 reduce-scatter.2.cloned.1.call-update
  202.1 3.2 copy.28
  205.3 2.6 copy.29
  207.8 3.7 all-to-all-start.1
  211.5 4.4 %copy.25 = bf16[256,5120]{0,1:T(8,128)(2,1)} copy(bf16[256,5120]{1,0:T(8,128)(2,1)} %param.6) | data formatting | bytes 5242880 | tf_op args[0]
  215.9 4.4 %copy.26 = bf16[256,4,1280]{2,0,1:T(8,128)(2,1)} copy(bf16[256,4,1280]{0,2,1:T(8,128)(2,1)} %bitcast.30) | data formatting | bytes 5242880 | tf_op jit(solution)/shard_map/all_to_all | solution.py:39
  220.3 41.8 %all-to-all-done.1 = bf16[256,4,1280]{2,0,1:T(8,128)(2,1)S(1)} async-done(((bf16[256,4,1280]{2,0,1:T(8,128)(2,1)}), bf16[256,4,1280]{2,0,1:T(8,128)(2,1)S(1)}, u32[]{:S(2)}, u32[]{:S(2)}) %all-to-all-start.1) | async-done | bytes 2621472 | tf_op jit(solution)/shard_map/all_to_all | solution.py:40
  262.1 4.5 %all-to-all-start = ((bf16[256,4,1280]{2,0,1:T(8,128)(2,1)}), bf16[256,4,1280]{2,0,1:T(8,128)(2,1)}, u32[]{:S(2)}, u32[]{:S(2)}) async-start(bf16[256,4,1280]{2,0,1:T(8,128)(2,1)} %copy.26), calls=%async_computation.1 | async-start | bytes 5242880 | tf_op jit(solution)/shard_map/all_to_all | solution.py:39
  266.7 0.2 all-gather.9.cloned.1.call-start
  266.9 0.0 all-gather.11.cloned.1.call-done
  266.9 7.9 %copy.23 = bf16[1024,2688]{1,0:T(8,128)(2,1)} copy(bf16[1024,2688]{0,1:T(8,128)(2,1)} %all-gather.11.cloned.1.call-done) | data formatting | bytes 11010048 | tf_op jit(solution)/shard_map/all_gather | solution.py:43
  274.8 7.7 %fusion.1 = bf16[4,1280,896]{1,2,0:T(8,128)(2,1)} fusion(bf16[256,4,1280]{2,0,1:T(8,128)(2,1)S(1)} %all-to-all-done.1, bf16[4,256,2688]{2,1,0:T(8,128)(2,1)} %bitcast.27), kind=kOutput, calls=%fused_computation.5 | convolution fusion | flops 2353397760 | bytes 13631488 | tf_op jit(solution)/shard_map/gtn,gtk->gnk/dot_general | solution.py:54
  282.5 15.5 %all-to-all-done = bf16[256,4,1280]{2,0,1:T(8,128)(2,1)} async-done(((bf16[256,4,1280]{2,0,1:T(8,128)(2,1)}), bf16[256,4,1280]{2,0,1:T(8,128)(2,1)}, u32[]{:S(2)}, u32[]{:S(2)}) %all-to-all-start) | async-done | bytes 2621472 | tf_op jit(solution)/shard_map/all_to_all | solution.py:39
  298.0 11.2 %fusion = bf16[4,1280,1792]{1,2,0:T(8,128)(2,1)} fusion(bf16[4,256,2688]{2,1,0:T(8,128)(2,1)} %bitcast.28, bf16[256,4,1280]{2,0,1:T(8,128)(2,1)} %all-to-all-done), kind=kOutput, calls=%fused_computation.3 | convolution fusion | flops 4706795520 | bytes 24641536 | tf_op jit(solution)/shard_map/gtn,gtk->gnk/dot_general | solution.py:48
  309.2 21.9 %reduce-scatter.2.cloned.1.call-done = bf16[32,5120]{1,0:T(8,128)(2,1)} async-done(((bf16[256,5120]{1,0:T(8,128)(2,1)}), bf16[32,5120]{1,0:T(8,128)(2,1)}) %reduce-scatter.2.cloned.1.call-update) | async-done | bytes 327696 | tf_op jit(solution)/shard_map/reduce_scatter | solution.py:34
  331.1 0.0 all-gather.9.cloned.1.call-update
  331.1 19.5 %pad_maximum_fusion = bf16[4,1280,2688]{1,2,0:T(8,128)(2,1)} fusion(bf16[4,1280,896]{1,2,0:T(8,128)(2,1)} %fusion.1, bf16[4,1280,1792]{1,2,0:T(8,128)(2,1)} %fusion), kind=kLoop, calls=%fused_computation.2 | loop fusion | flops 55050240 | bytes 55050240 | tf_op jit(solution)/shard_map/concatenate | solution.py:60
  350.6 15.2 %convert_reduce_fusion = f32[1280,2688]{0,1:T(8,128)} fusion(bf16[4,1280,2688]{1,2,0:T(8,128)(2,1)} %pad_maximum_fusion), kind=kLoop, calls=%fused_computation | loop fusion | flops 24084480 | bytes 41287680 | tf_op jit(solution)/shard_map/reduce_sum | solution.py:62
  365.8 10.6 %broadcast_multiply_fusion = f32[1280,2688]{0,1:T(8,128)} fusion(f32[1280,2688]{0,1:T(8,128)} %convert_reduce_fusion), kind=kLoop, calls=%fused_computation.6 | loop fusion | flops 3440640 | bytes 27525120 | tf_op jit(solution)/shard_map/div | solution.py:63
  376.4 7.9 %slice.18 = f32[1280,1792]{0,1:T(8,128)} slice(f32[1280,2688]{0,1:T(8,128)} %broadcast_multiply_fusion), slice={[0:1280], [0:1792]} | slice | bytes 18350080 | tf_op jit(solution)/shard_map/slice | solution.py:64
  384.3 4.8 %slice.19 = f32[1280,896]{0,1:T(8,128)} slice(f32[1280,2688]{0,1:T(8,128)} %broadcast_multiply_fusion), slice={[0:1280], [1792:2688]} | slice | bytes 9175040 | tf_op jit(solution)/shard_map/slice | solution.py:65
  389.1 16.1 %copy.30 = f32[1280,2,896]{2,1,0:T(2,128)} copy(f32[1280,2,896]{0,2,1:T(8,128)} %bitcast.26) | data formatting | bytes 18350080
  405.2 5.7 %copy.31 = f32[1280,896]{1,0:T(8,128)} copy(f32[1280,896]{0,1:T(8,128)} %slice.19) | data formatting | bytes 9175040
  410.9 0.0 all-gather.9.cloned.1.call-done
  410.9 3.4 copy.35
Async XLA Ops:
  7.2 67.8 %all-gather.5.cloned.1.call-start = ((), (), s32[]{:S(2)}) async-start(), calls=%async_computation.3 | async-start | bytes 11468800 | tf_op jit(solution)/shard_map/all_gather | solution.py:19
  7.9 5.2 %copy-start.3 = (bf16[256,896]{1,0:T(8,128)(2,1)S(1)}, bf16[256,896]{1,0:T(8,128)(2,1)}, u32[]{:S(2)}) copy-start(bf16[256,896]{1,0:T(8,128)(2,1)} %param.9) | copy-start | bytes 1376260
  7.9 184.3 %all-gather.7.cloned.1.call-start = ((), (), s32[]{:S(2)}) async-start(), calls=%async_computation.4 | async-start | bytes 22937600 | tf_op jit(solution)/shard_map/all_gather | solution.py:29
  13.0 62.0 %copy-start = (bf16[256,5120]{1,0:T(8,128)(2,1)S(1)}, bf16[256,5120]{1,0:T(8,128)(2,1)}, u32[]{:S(2)}) copy-start(bf16[256,5120]{1,0:T(8,128)(2,1)} %param.7) | copy-start | bytes 7864324
  13.0 253.9 %all-gather.11.cloned.1.call-start = ((), (), s32[]{:S(2)}) async-start(), calls=%async_computation.7 | async-start | bytes 6881280 | tf_op jit(solution)/shard_map/all_gather | solution.py:43
  82.0 0.8 copy-start.1
  82.8 109.4 %copy-start.2 = (bf16[256,1,896]{2,0,1:T(8,128)(2,1)S(1)}, bf16[256,1,896]{2,0,1:T(8,128)(2,1)}, u32[]{:S(2)}) copy-start(bf16[256,1,896]{2,0,1:T(8,128)(2,1)} %copy-done.1) | copy-start | bytes 1376260
  84.6 246.5 %reduce-scatter.2.cloned.1.call-start = ((), (), s32[]{:S(2)}) async-start(), calls=%async_computation.5 | async-start | bytes 2949120 | tf_op jit(solution)/shard_map/reduce_scatter | solution.py:34
  207.8 54.3 %all-to-all-start.1 = ((bf16[256,4,1280]{2,0,1:T(8,128)(2,1)}), bf16[256,4,1280]{2,0,1:T(8,128)(2,1)S(1)}, u32[]{:S(2)}, u32[]{:S(2)}) async-start(bf16[256,4,1280]{2,0,1:T(8,128)(2,1)} %copy.29), calls=%async_computation.2 | async-start | bytes 5242880 | tf_op jit(solution)/shard_map/all_to_all | solution.py:40
  262.1 35.9 %all-to-all-start = ((bf16[256,4,1280]{2,0,1:T(8,128)(2,1)}), bf16[256,4,1280]{2,0,1:T(8,128)(2,1)}, u32[]{:S(2)}, u32[]{:S(2)}) async-start(bf16[256,4,1280]{2,0,1:T(8,128)(2,1)} %copy.26), calls=%async_computation.1 | async-start | bytes 5242880 | tf_op jit(solution)/shard_map/all_to_all | solution.py:39
  266.7 144.2 %all-gather.9.cloned.1.call-start = ((), (), s32[]{:S(2)}) async-start(), calls=%async_computation.6 | async-start | bytes 2949120 | tf_op jit(solution)/shard_map/all_gather | solution.py:37
Sparse Core Ops, SparseCore 0:
  9.5 65.4 all-gather.4
  77.2 115.0 all-gather.6
  193.8 62.0 all-gather.10
  259.8 71.3 reduce-scatter.1
  333.1 53.4 all-gather.8
where the time goes:
time: 422 us; the launch traced here: 421 us
  waiting for transfers between devices  248 us (59%)
  local copies, waits for them, and re-layouts  66.8 us (16%)
  other arithmetic  48 us (11%)
  matrix products  35.7 us (8%)
  between operations  13.9 us (3%)
  starting transfers between devices  8.59 us (2%)
    all_gather x1, waiting for transfers between devices, per_device(): pieces = lax.all_gather(gate_up, 'dp', axis=0, tiled=True)  108 us
    all_gather x1, waiting for transfers between devices, per_device(): lax.all_gather(down_weight, 'dp', axis=0, tiled=True)  60.2 us
    all_to_all x1, waiting for transfers between devices, per_device(): lax.all_to_all(grad_out, 'dp', split_axis=1, concat_axis=0, tiled=True)  41.8 us
    unnamed x14, local copies, waits for them, and re-layouts  38.6 us
    reduce_scatter x1, waiting for transfers between devices, per_device(): lax.psum_scatter(partial_sum.astype(jnp.bfloat16), 'tensor', scatter_dime...  21.9 us
    concatenate x1, other arithmetic, per_device(): paired = jnp.concatenate([gate_part, down_part], axis=2)  19.5 us
    all_to_all x1, waiting for transfers between devices, per_device(): lax.all_to_all(activations, 'dp', split_axis=1, concat_axis=0, tiled=True)  15.5 us
    reduce_sum x1, other arithmetic, per_device(): summed = jnp.sum(paired.astype(jnp.float32), axis=0)  15.2 us
  transfers between devices with their start and end apart: 7, of which 5 were waited for; matrix products, arithmetic and copies ran while one was open for 35% of the time, Pallas kernels for 0%

commit v1 on v0

v1 whole, which is shorter than its diff:
```python
import jax
import jax.numpy as jnp
from jax import lax
from jax.experimental import pallas as pl
from jax.experimental.pallas import tpu as pltpu
from jax.sharding import PartitionSpec as P

MESH = pl.DeviceIdType.MESH
ANY = pl.BlockSpec(memory_space=pl.ANY)
VMEM = pl.BlockSpec(memory_space=pltpu.VMEM)


def remote(src, dst, send, recv, device):
    return pltpu.make_async_remote_copy(
        src_ref=src, dst_ref=dst, send_sem=send, recv_sem=recv, device_id=device, device_id_type=MESH
    )


def greet(axes):
    barrier = pltpu.get_barrier_semaphore()
    count = 0
    for axis in axes:
        n = lax.axis_size(axis)
        me = lax.axis_index(axis)
        for s in range(1, n):
            pl.semaphore_signal(
                barrier, inc=1, device_id={axis: lax.rem(me + s, n)}, device_id_type=MESH
            )
        count += n - 1
    pl.semaphore_wait(barrier, count)


def spread(cid, block, wide=()):
    n = lax.axis_size("dp")
    m = lax.axis_size("tensor")
    w = len(wide)
    rows, width = block.shape[1:]

    def kernel(*refs):
        block_ref = refs[0]
        wide_refs = refs[1 : 1 + w]
        out_ref = refs[1 + w]
        wide_outs = refs[2 + w : 2 + 2 * w]
        s1, r1, s2, r2, sw, rw, local = refs[2 + 2 * w :]
        me = lax.axis_index("dp")
        j = lax.axis_index("tensor")
        partner = me + 1 - 2 * lax.rem(me, 2)
        greet(("dp", "tensor"))
        sends = []
        for s in range(1, n):
            p = lax.rem(me + s, n)
            sends.append(
                remote(block_ref.at[p], out_ref.at[me, j], s1.at[s], r1.at[me], {"dp": p})
            )
            sends[-1].start()
        locals_ = [pltpu.make_async_copy(block_ref.at[me], out_ref.at[me, j], local.at[w])]
        locals_[-1].start()
        for a in range(w):
            for s in range(1, n // 2):
                q = lax.rem(me + 2 * s, n)
                sends.append(
                    remote(wide_refs[a], wide_outs[a].at[me], sw.at[a, s], rw.at[a, me], {"dp": q})
                )
                sends[-1].start()
        for a in range(w):
            sends.append(
                remote(wide_refs[a], wide_outs[a].at[me], sw.at[a, 0], rw.at[a, me], {"dp": partner})
            )
            sends[-1].start()
            locals_.append(pltpu.make_async_copy(wide_refs[a], wide_outs[a].at[me], local.at[a]))
            locals_[-1].start()
        for s in range(1, n):
            p = lax.rem(me + n - s, n)
            remote(block_ref.at[p], out_ref.at[p, j], s1.at[s], r1.at[p], {"dp": p}).wait_recv()
        locals_[0].wait()
        for s in range(1, m):
            k = lax.rem(j + s, m)
            sends.append(
                remote(out_ref.at[:, j], out_ref.at[:, j], s2.at[s], r2.at[j], {"tensor": k})
            )
            sends[-1].start()
        for a in range(w):
            for s in range(1, n // 2):
                q = lax.rem(me + n - 2 * s, n)
                remote(
                    wide_refs[a], wide_outs[a].at[q], sw.at[a, s], rw.at[a, q], {"dp": q}
                ).wait_recv()
                sends.append(
                    remote(
                        wide_outs[a].at[q],
                        wide_outs[a].at[q],
                        sw.at[a, n // 2 + s - 1],
                        rw.at[a, q],
                        {"dp": partner},
                    )
                )
                sends[-1].start()
        for a in range(w):
            locals_[1 + a].wait()
            for s in range(n // 2):
                q = lax.rem(partner + 2 * s, n)
                remote(
                    wide_refs[a], wide_outs[a].at[q], sw.at[a, s], rw.at[a, q], {"dp": partner}
                ).wait_recv()
        for s in range(1, m):
            k = lax.rem(j + m - s, m)
            remote(
                out_ref.at[:, k], out_ref.at[:, k], s2.at[s], r2.at[k], {"tensor": k}
            ).wait_recv()
        for copy in sends:
            copy.wait_send()

    dma = pltpu.SemaphoreType.DMA
    shapes = [jax.ShapeDtypeStruct((n, m, rows, width), block.dtype)]
    shapes += [jax.ShapeDtypeStruct((n,) + a.shape, a.dtype) for a in wide]
    return pl.pallas_call(
        kernel,
        out_shape=shapes,
        in_specs=[VMEM] * (1 + w),
        out_specs=[ANY] * (1 + w),
        scratch_shapes=[
            dma((n,)),
            dma((n,)),
            dma((m,)),
            dma((m,)),
            dma((max(w, 1), n)),
            dma((max(w, 1), n)),
            dma((w + 1,)),
        ],
        compiler_params=pltpu.CompilerParams(collective_id=cid, has_side_effects=True),
    )(block, *wide)


def trade(cid, parts):
    n, m, rows, width = parts.shape

    def kernel(src, dst, send, recv, local):
        j = lax.axis_index("tensor")
        greet(("tensor",))
        sends = []
        for s in range(1, m):
            k = lax.rem(j + s, m)
            sends.append(remote(src.at[:, k], dst.at[j], send.at[s], recv.at[j], {"tensor": k}))
            sends[-1].start()
        own = pltpu.make_async_copy(src.at[:, j], dst.at[j], local)
        own.start()
        for s in range(1, m):
            k = lax.rem(j + m - s, m)
            remote(src.at[:, k], dst.at[k], send.at[s], recv.at[k], {"tensor": k}).wait_recv()
        own.wait()
        for copy in sends:
            copy.wait_send()

    dma = pltpu.SemaphoreType.DMA
    return pl.pallas_call(
        kernel,
        out_shape=jax.ShapeDtypeStruct((m, n, rows, width), parts.dtype),
        in_specs=[ANY],
        out_specs=ANY,
        scratch_shapes=[dma((m,)), dma((m,)), dma],
        compiler_params=pltpu.CompilerParams(collective_id=cid, has_side_effects=True),
    )(parts)


def add_over_dp(partial):
    n = partial.shape[0]
    me = lax.axis_index("dp")
    core = lax.rem(me, 2)
    pairs = partial.reshape((n // 2, 2) + partial.shape[1:])
    other = lax.dynamic_index_in_dim(pairs, 1 - core, 1, keepdims=False).astype(jnp.bfloat16)
    keep = lax.dynamic_index_in_dim(pairs, core, 1, keepdims=False)
    came = lax.ppermute(other, "dp", [(i, i ^ 1) for i in range(n)])
    half = keep + came.astype(jnp.float32)
    mine = me // 2
    total = lax.dynamic_index_in_dim(half, mine, 0, keepdims=False)
    for s in range(1, n // 2):
        piece = lax.dynamic_index_in_dim(half, lax.rem(mine + s, n // 2), 0, keepdims=False)
        came = lax.ppermute(
            piece.astype(jnp.bfloat16), "dp", [(i, (i + 2 * s) % n) for i in range(n)]
        )
        total = total + came.astype(jnp.float32)
    return total.astype(jnp.bfloat16)


def per_device(activations, grad_out, gate_pre, up_pre, gate_up, down_weight):
    tokens, model = activations.shape
    slab, hidden_width = down_weight.shape
    n = lax.axis_size("dp")
    m = lax.axis_size("tensor")
    rows = tokens // m
    j = lax.axis_index("tensor")

    def own_rows(a):
        piece = lax.dynamic_slice_in_dim(a, j * rows, rows, 0)
        return piece.reshape(rows, n, slab).transpose(1, 0, 2)

    dy, gate_all, up_all = spread(1, own_rows(grad_out), (gate_pre, up_pre))
    dy_cols = dy.reshape(n * tokens, slab)
    partial = jnp.dot(dy_cols, down_weight, preferred_element_type=jnp.float32)
    grad_h = add_over_dp(partial.reshape(n, tokens, hidden_width))
    x, grad_h_all = spread(2, own_rows(activations), (grad_h,))
    x_cols = x.reshape(n * tokens, slab)

    def flat(a):
        return a.reshape(n * tokens, hidden_width).astype(jnp.float32)

    gate_wide, up_wide, grad_h = flat(gate_all), flat(up_all), flat(grad_h_all)
    gate_sigmoid = jax.nn.sigmoid(gate_wide)
    gate_silu = gate_wide * gate_sigmoid
    hidden = (gate_silu * up_wide).astype(jnp.bfloat16)
    grad_gate = grad_h * up_wide * gate_sigmoid * (1.0 + gate_wide * (1.0 - gate_sigmoid))
    grad_gate = grad_gate.astype(jnp.bfloat16)
    grad_up = (grad_h * gate_silu).astype(jnp.bfloat16)
    grad_hidden = jnp.concatenate([grad_gate, grad_up], axis=1)

    part = lax.dot_general(
        grad_hidden,
        gate_up.reshape(slab, 2 * hidden_width),
        (((1,), (1,)), ((), ())),
        preferred_element_type=jnp.float32,
    ).astype(jnp.bfloat16)
    parts = trade(3, part.reshape(n, m, rows, slab))
    summed = jnp.sum(parts.astype(jnp.float32), axis=0).astype(jnp.bfloat16)
    (gathered,) = spread(4, summed)
    grad_input = gathered.transpose(1, 2, 0, 3).reshape(tokens, model)

    def weight(a, b):
        total = lax.dot_general(
            a, b, (((0,), (0,)), ((), ())), preferred_element_type=jnp.float32
        )
        return total / n

    grad_gate_up = jnp.stack([weight(x_cols, grad_gate), weight(x_cols, grad_up)], axis=1)
    grad_down = weight(dy_cols, hidden)
    return (grad_input, grad_gate_up, grad_down)


def solution(mesh):
    in_specs = (
        P("dp", None),
        P("dp", None),
        P("dp", "tensor"),
        P("dp", "tensor"),
        P("dp", None, "tensor"),
        P("dp", "tensor"),
    )
    out_specs = (P("dp", None), P("dp", None, "tensor"), P("dp", "tensor"))
    return jax.shard_map(
        per_device, mesh=mesh, in_specs=in_specs, out_specs=out_specs, check_vma=False
    )
```

time: 422 us -> 349 us (0.83)
  the two profiles are of different devices: /device:TPU:0 before, /device:TPU:13 now
where the time goes in v1:
time: 349 us
  Pallas kernels  266 us (76%)
  local copies, waits for them, and re-layouts  32.6 us (9%)
  matrix products  24.7 us (7%)
  other arithmetic  17.6 us (5%)
  waiting for transfers between devices  6.67 us (2%)
    pallas_call x3, Pallas kernels, spread(): pl.pallas_call(kernel, out_shape=shapes, in_specs=[VMEM] * (1 + w), out_s...  205 us
    pallas_call x1, Pallas kernels, trade(): pl.pallas_call(kernel, out_shape=jax.ShapeDtypeStruct((m, n, rows, width)...  60.9 us
    unnamed x29, local copies, waits for them, and re-layouts  24.4 us
    dot_general x3, matrix products, weight(): lax.dot_general(a, b, (((0,), (0,)), ((), ())), preferred_element_type=jn...  12.1 us
  transfers between devices with their start and end apart: 2, of which 2 were waited for; matrix products, arithmetic and copies ran while one was open for 2% of the time, Pallas kernels for 0%

profile of v1, /device:TPU:13, one launch (start us, length us, event | category | flops | bytes accessed | tf_op | source)
XLA Modules:
  0.0 348.8 jit_solution(1822403558649449489)
XLA Ops:
  0.6 0.0 copy-start
  0.7 1.3 constant_dynamic-slice_fusion
  1.9 0.7 copy.24
  2.7 68.9 %shard_map.85 = (bf16[4,8,32,1280]{3,2,1,0:T(8,128)(2,1)}, bf16[4,256,896]{2,1,0:T(8,128)(2,1)}, bf16[4,256,896]{2,1,0:T(8,128)(2,1)}) custom-call(bf16[4,32,1280]{2,1,0:T(8,128)(2,1)} %bitcast.104, bf16[256,896]{1,0:T(8,128)(2,1)} %refs_1_.1, bf16[256,896]{1,0:T(8,128)(2,1)} %refs_2_.1), custom_call_target="tpu_custom_call" | custom-call | tf_op jit(solution)/shard_map/pallas_call | solution.py:116
  71.6 0.0 copy-done
  71.6 6.4 %fusion.20 = f32[2,2,256,896]{3,2,1,0:T(8,128)} fusion(bf16[2,2,256,1280]{3,2,1,0:T(8,128)(2,1)} %bitcast.106, bf16[1280,896]{1,0:T(8,128)(2,1)S(1)} %copy-done), kind=kOutput, calls=%fused_computation.35 | convolution fusion | flops 2348810240 | bytes 8585216 | tf_op jit(solution)/shard_map/dot_general | solution.py:199
  78.0 1.6 fusion.22
  79.6 0.5 collective-permute-start
  80.1 2.1 collective-permute-done
  82.2 1.7 bitcast_add_fusion
  83.9 0.0 copy-start.5
  83.9 0.1 fusion.24
  83.9 0.3 collective-permute-start.1
  84.3 0.8 copy-done.5
  85.1 5.3 %copy.20 = bf16[160,8,2,896]{3,1,2,0:T(8,128)(2,1)} copy(bf16[160,8,2,896]{3,2,1,0:T(2,128)(2,1)} %bitcast.93) | data formatting | bytes 9175040
  90.4 0.0 copy-start.2
  90.4 0.7 copy.25
  91.1 4.6 %collective-permute-done.1 = bf16[256,896]{1,0:T(8,128)(2,1)S(1)} collective-permute-done((bf16[256,896]{1,0:T(8,128)(2,1)S(1)}, bf16[256,896]{1,0:T(8,128)(2,1)S(1)}, u32[]{:S(2)}, u32[]{:S(2)}) %collective-permute-start.1) | collective-permute-done | bytes 458784 | tf_op jit(solution)/shard_map/ppermute | solution.py:178
  95.7 2.0 fusion.23.refs_1_
  97.7 67.6 %shard_map.86 = (bf16[4,8,32,1280]{3,2,1,0:T(8,128)(2,1)}, bf16[4,256,896]{2,1,0:T(8,128)(2,1)}) custom-call(bf16[4,32,1280]{2,1,0:T(8,128)(2,1)} %bitcast.102, bf16[256,896]{1,0:T(8,128)(2,1)} %fusion.23.refs_1_), custom_call_target="tpu_custom_call" | custom-call | tf_op jit(solution)/shard_map/pallas_call | solution.py:116
  165.4 0.0 copy-done.2
  165.4 0.0 copy-start.3
  165.4 0.0 copy-start.4
  165.4 0.0 slice-start
  165.4 3.8 %fusion.14 = (bf16[1024,896]{1,0:T(8,128)(2,1)S(1)}, bf16[1024,896]{1,0:T(8,128)(2,1)S(1)}) fusion(bf16[4,256,896]{2,1,0:T(8,128)(2,1)S(1)} %copy-done.2, bf16[4,256,896]{2,1,0:T(8,128)(2,1)} %get-tuple-element.9, bf16[4,256,896]{2,1,0:T(8,128)(2,1)} %get-tuple-element.10), kind=kLoop, calls=%fused_computation.25 | loop fusion | flops 14680064 | bytes 9175040 | tf_op jit(solution)/shard_map/convert_element_type | solution.py:212
  169.3 0.0 copy-done.3
  169.3 0.0 copy-done.4
  169.3 0.0 slice-start.1
  169.3 4.3 %multiply_convert_fusion = (bf16[4,256,896]{2,1,0:T(8,128)(2,1)}, bf16[4,256,896]{2,1,0:T(8,128)(2,1)}, bf16[4,256,896]{2,1,0:T(8,128)(2,1)}) fusion(bf16[4,256,896]{2,1,0:T(8,128)(2,1)S(1)} %copy-done.3, bf16[4,256,896]{2,1,0:T(8,128)(2,1)S(1)} %copy-done.2, bf16[4,256,896]{2,1,0:T(8,128)(2,1)S(1)} %copy-done.4), kind=kLoop, calls=%fused_computation.34 | loop fusion | flops 16515072 | bytes 11010048 | tf_op jit(solution)/shard_map/convert_element_type | solution.py:210
  173.6 0.0 slice-done
  173.6 0.0 slice-done.1
  173.6 6.2 %convolution_convert_fusion = bf16[1024,1280]{1,0:T(8,128)(2,1)} fusion(bf16[1280,1792]{1,0:T(8,128)(2,1)S(1)} %bitcast.96, bf16[1024,896]{1,0:T(8,128)(2,1)S(1)} %get-tuple-element.23, bf16[1024,896]{1,0:T(8,128)(2,1)S(1)} %get-tuple-element.22), kind=kOutput, calls=%fused_computation.4 | convolution fusion | flops 4706271232 | bytes 10878976 | tf_op jit(solution)/shard_map/dot_general | solution.py:216
  179.9 60.9 %shard_map.87 = bf16[8,4,32,1280]{3,2,1,0:T(8,128)(2,1)} custom-call(bf16[4,8,32,1280]{3,2,1,0:T(8,128)(2,1)} %bitcast.98), custom_call_target="tpu_custom_call" | custom-call | tf_op jit(solution)/shard_map/pallas_call | solution.py:155
  240.7 2.9 reduce_sum.12.refs_0_
  243.7 68.1 %shard_map.88 = bf16[4,8,32,1280]{3,2,1,0:T(8,128)(2,1)} custom-call(bf16[4,32,1280]{2,1,0:T(8,128)(2,1)} %reduce_sum.12.refs_0_), custom_call_target="tpu_custom_call" | custom-call | tf_op jit(solution)/shard_map/pallas_call | solution.py:116
  311.8 3.8 %copy.14 = bf16[8,32,4,1280]{3,2,1,0:T(4,128)(2,1)S(1)} copy(bf16[8,32,4,1280]{3,1,0,2:T(8,128)(2,1)} %bitcast.91) | data formatting | bytes 5242880 | tf_op jit(solution)/shard_map/transpose | solution.py:225
  315.5 0.0 copy-start.8
  315.6 0.0 copy-start.10
  315.6 2.0 copy.21
  317.5 0.0 copy-done.8
  317.5 1.3 copy-done.10
  318.8 0.0 copy-start.7
  318.8 3.0 multiply_bitcast_fusion
  321.8 0.0 copy-done.7
  321.8 4.5 %multiply_bitcast_fusion.1 = f32[1280,1,896]{2,0,1:T(8,128)} fusion(bf16[1024,1280]{1,0:T(8,128)(2,1)S(1)} %bitcast.109, bf16[1024,896]{1,0:T(8,128)(2,1)S(1)} %bitcast.100), kind=kOutput, calls=%fused_computation.2 | convolution fusion | flops 2349957120 | bytes 9043968 | tf_op jit(solution)/shard_map/dot_general | solution.py:228
  326.3 2.9 pad_maximum_fusion
  329.2 0.0 copy-start.6
  329.2 0.0 copy-start.9
  329.2 15.0 %copy.15 = f32[1280,2,896]{2,1,0:T(2,128)} copy(f32[1280,2,896]{2,0,1:T(8,128)S(1)} %pad_maximum_fusion) | data formatting | bytes 18350080
  344.2 0.0 copy-done.6
  344.2 0.0 copy-done.9
  344.2 0.0 copy-start.1
  344.2 4.5 %convolution_multiply_fusion = f32[1280,896]{1,0:T(8,128)} fusion(bf16[1024,1280]{1,0:T(8,128)(2,1)S(1)} %bitcast.107, bf16[1024,896]{1,0:T(8,128)(2,1)S(1)} %bitcast.99), kind=kOutput, calls=%fused_computation.3 | convolution fusion | flops 2349957120 | bytes 9043968 | tf_op jit(solution)/shard_map/dot_general | solution.py:228
  348.8 0.0 copy-done.1
  (1 shorter events, 0.0 us)
Async XLA Ops:
  0.6 71.0 %copy-start = (bf16[1280,896]{1,0:T(8,128)(2,1)S(1)}, bf16[1280,896]{1,0:T(8,128)(2,1)}, u32[]{:S(2)}) copy-start(bf16[1280,896]{1,0:T(8,128)(2,1)} %param.11) | copy-start | bytes 6881284
  79.6 2.6 collective-permute-start
  83.9 1.2 copy-start.5
  83.9 11.8 %collective-permute-start.1 = (bf16[256,896]{1,0:T(8,128)(2,1)S(1)}, bf16[256,896]{1,0:T(8,128)(2,1)S(1)}, u32[]{:S(2)}, u32[]{:S(2)}) collective-permute-start(bf16[256,896]{1,0:T(8,128)(2,1)S(1)} %fusion.24), channel_id=1, source_target_pairs={{0,16},{8,24},{16,0},{24,8},{1,17},{9,25},{17,1},{25,9},{2,18},{10... | collective-permute-start | bytes 1376264 | tf_op jit(solution)/shard_map/ppermute | solution.py:178
  90.4 75.0 %copy-start.2 = (bf16[4,256,896]{2,1,0:T(8,128)(2,1)S(1)}, bf16[4,256,896]{2,1,0:T(8,128)(2,1)}, u32[]{:S(2)}) copy-start(bf16[4,256,896]{2,1,0:T(8,128)(2,1)} %get-tuple-element.11) | copy-start | bytes 5505028
  165.4 3.9 %copy-start.3 = (bf16[4,256,896]{2,1,0:T(8,128)(2,1)S(1)}, bf16[4,256,896]{2,1,0:T(8,128)(2,1)}, u32[]{:S(2)}) copy-start(bf16[4,256,896]{2,1,0:T(8,128)(2,1)} %get-tuple-element.10) | copy-start | bytes 5505028
  165.4 3.9 %copy-start.4 = (bf16[4,256,896]{2,1,0:T(8,128)(2,1)S(1)}, bf16[4,256,896]{2,1,0:T(8,128)(2,1)}, u32[]{:S(2)}) copy-start(bf16[4,256,896]{2,1,0:T(8,128)(2,1)} %get-tuple-element.9) | copy-start | bytes 5505028
  165.4 8.2 %slice-start = ((s8[4587520]{0:T(1024)(128)(4,1)}), s8[4194304]{0:T(1024)(128)(4,1)S(1)}, s32[]{:S(2)}) async-start(s8[4587520]{0:T(1024)(128)(4,1)} %bitcast.94), calls=%async_computation | async-start | bytes 8388608
  169.3 4.3 %slice-start.1 = ((s8[4587520]{0:T(1024)(128)(4,1)}), s8[393216]{0:T(1024)(128)(4,1)S(1)}, s32[]{:S(2)}) async-start(s8[4587520]{0:T(1024)(128)(4,1)} %bitcast.94), calls=%async_computation.1 | async-start | bytes 786432
  315.5 2.0 copy-start.8
  315.6 3.2 copy-start.10
  318.8 3.0 copy-start.7
  329.2 15.0 %copy-start.6 = (bf16[4,256,896]{2,1,0:T(8,128)(2,1)S(1)}, bf16[4,256,896]{2,1,0:T(8,128)(2,1)}, u32[]{:S(2)}) copy-start(bf16[4,256,896]{2,1,0:T(8,128)(2,1)} %get-tuple-element.19) | copy-start | bytes 5505028
  329.2 15.0 %copy-start.9 = (bf16[4,8,32,1280]{3,2,1,0:T(8,128)(2,1)S(1)}, bf16[4,8,32,1280]{3,2,1,0:T(8,128)(2,1)}, u32[]{:S(2)}) copy-start(bf16[4,8,32,1280]{3,2,1,0:T(8,128)(2,1)} %get-tuple-element.8) | copy-start | bytes 7864324
  344.2 4.5 %copy-start.1 = (bf16[1280,896]{1,0:T(8,128)(2,1)S(1)}, bf16[1280,896]{1,0:T(8,128)(2,1)}, u32[]{:S(2)}) copy-start(bf16[1280,896]{1,0:T(8,128)(2,1)} %param.11) | copy-start | bytes 6881284

commit v2 on v1

--- a/solution.py
+++ b/solution.py
@@ -73,12 +73,46 @@
             p = lax.rem(me + n - s, n)
             remote(block_ref.at[p], out_ref.at[p, j], s1.at[s], r1.at[p], {"dp": p}).wait_recv()
         locals_[0].wait()
-        for s in range(1, m):
-            k = lax.rem(j + s, m)
-            sends.append(
-                remote(out_ref.at[:, j], out_ref.at[:, j], s2.at[s], r2.at[j], {"tensor": k})
-            )
-            sends[-1].start()
+        lines = m // 2
+        row, column = j // 2, lax.rem(j, 2)
+        facing = j + 1 - 2 * column
+        first, last = row == 0, row == lines - 1
+
+        def hop(kind, r, device):
+            k = 2 * r + column
+            return remote(
+                out_ref.at[:, k], out_ref.at[:, k], s2.at[kind, r], r2.at[k], {"tensor": device}
+            )
+
+        def up(r):
+            return hop(0, r, lax.rem(j + 2, m))
+
+        def down(r):
+            return hop(1, r, lax.rem(j + m - 2, m))
+
+        def across(r):
+            return hop(2, r, facing)
+
+        for d in range(lines):
+            below, above = row - d, row + d
+
+            @pl.when(below >= 0)
+            def _():
+                if d > 0:
+                    up(below).wait_recv()
+                pl.when(jnp.logical_not(last))(lambda: up(below).start())
+                if d == 0:
+                    pl.when(jnp.logical_not(first))(lambda: down(row).start())
+                across(below).start()
+
+            if d > 0:
+
+                @pl.when(above < lines)
+                def _():
+                    down(above).wait_recv()
+                    pl.when(jnp.logical_not(first))(lambda: down(above).start())
+                    across(above).start()
+
         for a in range(w):
             for s in range(1, n // 2):
                 q = lax.rem(me + n - 2 * s, n)
@@ -102,11 +136,16 @@
                 remote(
                     wide_refs[a], wide_outs[a].at[q], sw.at[a, s], rw.at[a, q], {"dp": partner}
                 ).wait_recv()
-        for s in range(1, m):
-            k = lax.rem(j + m - s, m)
+        for r in range(lines):
+            k = 2 * r + 1 - column
             remote(
-                out_ref.at[:, k], out_ref.at[:, k], s2.at[s], r2.at[k], {"tensor": k}
+                out_ref.at[:, k], out_ref.at[:, k], s2.at[2, r], r2.at[k], {"tensor": facing}
             ).wait_recv()
+            across(r).wait_send()
+            went_up = jnp.logical_and(jnp.logical_not(last), r <= row)
+            went_down = jnp.logical_and(jnp.logical_not(first), r >= row)
+            pl.when(went_up)(lambda: up(r).wait_send())
+            pl.when(went_down)(lambda: down(r).wait_send())
         for copy in sends:
             copy.wait_send()
 
@@ -121,7 +160,7 @@
         scratch_shapes=[
             dma((n,)),
             dma((n,)),
-            dma((m,)),
+            dma((3, m // 2)),
             dma((m,)),
             dma((max(w, 1), n)),
             dma((max(w, 1), n)),
@@ -182,6 +221,31 @@
     return total.astype(jnp.bfloat16)
 
 
+def paired_weight(x_cols, grad_gate, grad_up, scale):
+    depth, slab = x_cols.shape
+    width = grad_gate.shape[1]
+    tile = 128 if slab % 128 == 0 else slab
+
+    def kernel(x_ref, gate_ref, up_ref, out_ref):
+        for i, ref in enumerate((gate_ref, up_ref)):
+            total = lax.dot_general(
+                x_ref[...], ref[...], (((0,), (0,)), ((), ())), preferred_element_type=jnp.float32
+            )
+            out_ref[:, i, :] = total / scale
+
+    whole = pl.BlockSpec((depth, width), lambda i: (0, 0))
+    return pl.pallas_call(
+        kernel,
+        grid=(slab // tile,),
+        out_shape=jax.ShapeDtypeStruct((slab, 2, width), jnp.float32),
+        in_specs=[pl.BlockSpec((depth, tile), lambda i: (0, i)), whole, whole],
+        out_specs=pl.BlockSpec((tile, 2, width), lambda i: (i, 0, 0)),
+        cost_estimate=pl.CostEstimate(
+            flops=4 * depth * slab * width, bytes_accessed=8 * slab * width, transcendentals=0
+        ),
+    )(x_cols, grad_gate, grad_up)
+
+
 def per_device(activations, grad_out, gate_pre, up_pre, gate_up, down_weight):
     tokens, model = activations.shape
     slab, hidden_width = down_weight.shape
@@ -230,7 +294,7 @@
         )
         return total / n
 
-    grad_gate_up = jnp.stack([weight(x_cols, grad_gate), weight(x_cols, grad_up)], axis=1)
+    grad_gate_up = paired_weight(x_cols, grad_gate, grad_up, float(n))
     grad_down = weight(dy_cols, hidden)
     return (grad_input, grad_gate_up, grad_down)
 

time: 349 us -> 264 us (0.76)
  the two profiles are of different devices: /device:TPU:13 before, /device:TPU:0 now
where the time goes in v2:
time: 264 us; the launch traced here: 263 us
  Pallas kernels  211 us (80%)
  local copies, waits for them, and re-layouts  17.7 us (7%)
  matrix products  15.3 us (6%)
  other arithmetic  10.4 us (4%)
  waiting for transfers between devices  7.05 us (3%)
    pallas_call x3, Pallas kernels, spread(): pl.pallas_call(kernel, out_shape=shapes, in_specs=[VMEM] * (1 + w), out_s...  153 us
    pallas_call x1, Pallas kernels, trade(): pl.pallas_call(kernel, out_shape=jax.ShapeDtypeStruct((m, n, rows, width)...  45.2 us
    pallas_call x1, Pallas kernels, paired_weight(): pl.pallas_call(kernel, grid=(slab // tile,), out_shape=jax.ShapeDtypeStru...  13.1 us
    unnamed x22, local copies, waits for them, and re-layouts  10.1 us
    ppermute x1, waiting for transfers between devices, add_over_dp(): lax.ppermute(piece.astype(jnp.bfloat16), 'dp', [(i, (i + 2 * s) % n) for...  7.05 us
    dot_general x1, matrix products, per_device(): lax.dot_general(grad_hidden, gate_up.reshape(slab, 2 * hidden_width), (((...  6.22 us
  transfers between devices with their start and end apart: 2, of which 1 were waited for; matrix products, arithmetic and copies ran while one was open for 5% of the time, Pallas kernels for 0%

profile of v2, /device:TPU:0, one launch (start us, length us, event | category | flops | bytes accessed | tf_op | source)
XLA Modules:
  0.0 263.1 jit_solution(10911394919055683646)
XLA Ops:
  0.6 0.0 copy-start
  0.7 1.3 constant_dynamic-slice_fusion
  1.9 0.7 copy.22
  2.7 49.0 %shard_map.85 = (bf16[4,8,32,1280]{3,2,1,0:T(8,128)(2,1)}, bf16[4,256,896]{2,1,0:T(8,128)(2,1)}, bf16[4,256,896]{2,1,0:T(8,128)(2,1)}) custom-call(bf16[4,32,1280]{2,1,0:T(8,128)(2,1)} %bitcast.85, bf16[256,896]{1,0:T(8,128)(2,1)} %refs_1_.1, bf16[256,896]{1,0:T(8,128)(2,1)} %refs_2_.1), custom_call_target="tpu_custom_call" | custom-call | tf_op jit(solution)/shard_map/pallas_call | solution.py:155
  51.7 0.0 copy-done
  51.7 4.6 %fusion.16 = f32[2,2,256,896]{3,2,1,0:T(8,128)S(1)} fusion(bf16[2,2,256,1280]{3,2,1,0:T(8,128)(2,1)} %bitcast.87, bf16[1280,896]{1,0:T(8,128)(2,1)S(1)} %copy-done), kind=kOutput, calls=%fused_computation.25 | convolution fusion | flops 2348810240 | bytes 8585216 | tf_op jit(solution)/shard_map/dot_general | solution.py:263
  56.3 0.0 copy-start.3
  56.3 1.8 copy-done.3
  58.1 1.0 fusion.18
  59.1 0.0 collective-permute-start
  59.1 0.8 copy.23
  59.9 0.0 copy-start.2
  59.9 5.4 %copy.18 = bf16[160,8,2,896]{3,1,2,0:T(8,128)(2,1)} copy(bf16[160,8,2,896]{3,2,1,0:T(2,128)(2,1)} %bitcast.76) | data formatting | bytes 9175040
  65.3 0.0 copy-done.2
  65.3 0.0 copy-start.4
  65.3 2.7 %fusion.15 = bf16[4,256,896]{2,1,0:T(8,128)(2,1)S(1)} fusion(bf16[4,256,896]{2,1,0:T(8,128)(2,1)S(1)} %copy-done.2, bf16[4,256,896]{2,1,0:T(8,128)(2,1)} %get-tuple-element.10), kind=kLoop, calls=%fused_computation.24 | loop fusion | flops 7340032 | bytes 5505024 | tf_op jit(solution)/shard_map/convert_element_type | solution.py:274
  68.1 0.0 copy-start.7
  68.1 0.0 collective-permute-done
  68.1 0.0 copy-done.4
  68.1 0.2 bitcast_add_fusion
  68.3 0.1 fusion.20
  68.4 0.6 collective-permute-start.1
  69.0 0.8 copy-done.7
  69.8 4.5 %convolution_multiply_fusion = f32[1280,896]{1,0:T(8,128)} fusion(bf16[1024,1280]{1,0:T(8,128)(2,1)S(1)} %bitcast.88, bf16[1024,896]{1,0:T(8,128)(2,1)S(1)} %bitcast.82), kind=kOutput, calls=%fused_computation.2 | convolution fusion | flops 2349957120 | bytes 9043968 | tf_op jit(solution)/shard_map/dot_general | solution.py:292
  74.3 7.0 %collective-permute-done.1 = bf16[256,896]{1,0:T(8,128)(2,1)S(1)} collective-permute-done((bf16[256,896]{1,0:T(8,128)(2,1)S(1)}, bf16[256,896]{1,0:T(8,128)(2,1)S(1)}, u32[]{:S(2)}, u32[]{:S(2)}) %collective-permute-start.1) | collective-permute-done | bytes 458784 | tf_op jit(solution)/shard_map/ppermute | solution.py:217
  81.4 0.9 fusion.19.refs_1_
  82.2 0.0 slice-start
  82.2 45.0 %shard_map.86 = (bf16[4,8,32,1280]{3,2,1,0:T(8,128)(2,1)}, bf16[4,256,896]{2,1,0:T(8,128)(2,1)}) custom-call(bf16[4,32,1280]{2,1,0:T(8,128)(2,1)} %bitcast.83, bf16[256,896]{1,0:T(8,128)(2,1)} %fusion.19.refs_1_), custom_call_target="tpu_custom_call" | custom-call | tf_op jit(solution)/shard_map/pallas_call | solution.py:155
  127.3 0.0 slice-start.1
  127.3 3.6 %fusion.2 = (bf16[1024,896]{1,0:T(8,128)(2,1)S(1)}, bf16[1024,896]{1,0:T(8,128)(2,1)S(1)}) fusion(bf16[4,256,896]{2,1,0:T(8,128)(2,1)S(1)} %copy-done.2, bf16[4,256,896]{2,1,0:T(8,128)(2,1)} %get-tuple-element.9, bf16[4,256,896]{2,1,0:T(8,128)(2,1)} %get-tuple-element.10), kind=kLoop, calls=%fused_computation.6 | loop fusion | flops 14680064 | bytes 9175040 | tf_op jit(solution)/shard_map/convert_element_type | solution.py:276
  130.9 0.0 copy-start.5
  130.9 0.0 copy-start.6
  130.9 0.0 slice-done
  131.0 0.0 slice-done.1
  131.0 6.2 %convolution_convert_fusion = bf16[1024,1280]{1,0:T(8,128)(2,1)} fusion(bf16[1280,1792]{1,0:T(8,128)(2,1)S(1)} %bitcast.79, bf16[1024,896]{1,0:T(8,128)(2,1)S(1)} %get-tuple-element.14.up_ref, bf16[1024,896]{1,0:T(8,128)(2,1)S(1)} %get-tuple-element.13.gate_ref), kind=kOutput, calls=%fused_computation.3 | convolution fusion | flops 4706271232 | bytes 10878976 | tf_op jit(solution)/shard_map/dot_general | solution.py:280
  137.2 0.0 copy-done.5
  137.2 0.0 copy-done.6
  137.2 45.2 %shard_map.87 = bf16[8,4,32,1280]{3,2,1,0:T(8,128)(2,1)} custom-call(bf16[4,8,32,1280]{3,2,1,0:T(8,128)(2,1)} %bitcast.81), custom_call_target="tpu_custom_call" | custom-call | tf_op jit(solution)/shard_map/pallas_call | solution.py:194
  182.4 2.9 %reduce_sum.12.refs_0_ = bf16[4,32,1280]{2,1,0:T(8,128)(2,1)} reduce(bf16[8,4,32,1280]{3,2,1,0:T(8,128)(2,1)} %shard_map.87, bf16[]{:T(256)} %constant.51.clone.1), dimensions={0}, to_apply=%region_0.1 | reduce | flops 1146880 | bytes 2949122 | tf_op jit(solution)/shard_map/reduce_sum | solution.py:287
  185.3 58.9 %shard_map.88 = bf16[4,8,32,1280]{3,2,1,0:T(8,128)(2,1)} custom-call(bf16[4,32,1280]{2,1,0:T(8,128)(2,1)} %reduce_sum.12.refs_0_), custom_call_target="tpu_custom_call" | custom-call | tf_op jit(solution)/shard_map/pallas_call | solution.py:155
  244.3 3.8 %copy.13 = bf16[8,32,4,1280]{3,2,1,0:T(4,128)(2,1)S(1)} copy(bf16[8,32,4,1280]{3,1,0,2:T(8,128)(2,1)} %bitcast.74) | data formatting | bytes 5242880 | tf_op jit(solution)/shard_map/transpose | solution.py:289
  248.0 2.0 copy.19
  250.0 0.0 copy-start.1
  250.0 13.1 %shard_map.89 = f32[1280,2,896]{2,1,0:T(2,128)} custom-call(bf16[1024,1280]{1,0:T(8,128)(2,1)} %bitcast.89, bf16[1024,896]{1,0:T(8,128)(2,1)} %copy-done.5, bf16[1024,896]{1,0:T(8,128)(2,1)} %copy-done.6), custom_call_target="tpu_custom_call" | custom-call | flops 4697620480 | bytes 9175040 | tf_op jit(solution)/shard_map/pallas_call | solution.py:237
  263.1 0.0 copy-done.1
  (1 shorter events, 0.0 us)
Async XLA Ops:
  0.6 51.0 %copy-start = (bf16[1280,896]{1,0:T(8,128)(2,1)S(1)}, bf16[1280,896]{1,0:T(8,128)(2,1)}, u32[]{:S(2)}) copy-start(bf16[1280,896]{1,0:T(8,128)(2,1)} %param.11) | copy-start | bytes 6881284
  56.3 1.8 copy-start.3
  59.1 9.0 %collective-permute-start = (bf16[2,256,896]{2,1,0:T(8,128)(2,1)}, bf16[2,256,896]{2,1,0:T(8,128)(2,1)S(1)}, u32[]{:S(2)}, u32[]{:S(2)}) collective-permute-start(bf16[2,256,896]{2,1,0:T(8,128)(2,1)} %fusion.18), channel_id=1, source_target_pairs={{0,8},{8,0},{16,24},{24,16},{1,9},{9,1},{17,25},{25,17},{2,10},{10... | collective-permute-start | bytes 2752520 | tf_op jit(solution)/shard_map/ppermute | solution.py:211
  59.9 5.4 %copy-start.2 = (bf16[4,256,896]{2,1,0:T(8,128)(2,1)S(1)}, bf16[4,256,896]{2,1,0:T(8,128)(2,1)}, u32[]{:S(2)}) copy-start(bf16[4,256,896]{2,1,0:T(8,128)(2,1)} %get-tuple-element.11) | copy-start | bytes 5505028
  65.3 2.8 %copy-start.4 = (f32[2,2,256,896]{3,2,1,0:T(8,128)S(1)}, f32[2,2,256,896]{3,2,1,0:T(8,128)}, u32[]{:S(2)}) copy-start(f32[2,2,256,896]{3,2,1,0:T(8,128)} %copy-done.3) | copy-start | bytes 11010052
  68.1 1.7 copy-start.7
  68.4 13.0 %collective-permute-start.1 = (bf16[256,896]{1,0:T(8,128)(2,1)S(1)}, bf16[256,896]{1,0:T(8,128)(2,1)S(1)}, u32[]{:S(2)}, u32[]{:S(2)}) collective-permute-start(bf16[256,896]{1,0:T(8,128)(2,1)S(1)} %fusion.20), channel_id=1, source_target_pairs={{0,16},{8,24},{16,0},{24,8},{1,17},{9,25},{17,1},{25,9},{2,18},{10... | collective-permute-start | bytes 1376264 | tf_op jit(solution)/shard_map/ppermute | solution.py:217
  82.2 48.7 %slice-start = ((s8[4587520]{0:T(1024)(128)(4,1)}), s8[393216]{0:T(1024)(128)(4,1)S(1)}, s32[]{:S(2)}) async-start(s8[4587520]{0:T(1024)(128)(4,1)} %bitcast.77), calls=%async_computation | async-start | bytes 786432
  127.3 3.7 %slice-start.1 = ((s8[4587520]{0:T(1024)(128)(4,1)}), s8[4194304]{0:T(1024)(128)(4,1)S(1)}, s32[]{:S(2)}) async-start(s8[4587520]{0:T(1024)(128)(4,1)} %bitcast.77), calls=%async_computation.1 | async-start | bytes 8388608
  130.9 6.3 %copy-start.5 = (bf16[1024,896]{1,0:T(8,128)(2,1)}, bf16[1024,896]{1,0:T(8,128)(2,1)S(1)}, u32[]{:S(2)}) copy-start(bf16[1024,896]{1,0:T(8,128)(2,1)S(1)} %get-tuple-element.13.gate_ref) | copy-start | bytes 5505028
  130.9 6.3 %copy-start.6 = (bf16[1024,896]{1,0:T(8,128)(2,1)}, bf16[1024,896]{1,0:T(8,128)(2,1)S(1)}, u32[]{:S(2)}) copy-start(bf16[1024,896]{1,0:T(8,128)(2,1)S(1)} %get-tuple-element.14.up_ref) | copy-start | bytes 5505028
  250.0 13.1 %copy-start.1 = (bf16[1280,896]{1,0:T(8,128)(2,1)S(1)}, bf16[1280,896]{1,0:T(8,128)(2,1)}, u32[]{:S(2)}) copy-start(bf16[1280,896]{1,0:T(8,128)(2,1)} %param.11) | copy-start | bytes 6881284
